TPU v7x, 128 devices: a whole 4x4x4 slice. The times are simulated.
128 devices in a mesh: row: 32 (over y, z, core), col: 4 (over x).
Axes of the slice: x: 4, y: 4, z: 4, core: 2. Of those that a mesh axis runs over, the one named last changes fastest.
Arguments:
- acts_in: bfloat16 [32768, 4608], P('row'), may hold values from -64 to 64
- grad_query: bfloat16 [32768, 4096], P('row', 'col'), may hold values from -1.41421356 to 1.41421356
- attn_out: bfloat16 [32768, 4096], P('row'), may hold values from -64 to 64
- grad_out: bfloat16 [32768, 4608], P('row', 'col'), may hold values from -1.41421356 to 1.41421356
- row_query: float32 [4608], P('row'), may hold values from 0.05 to 18
- col_query: float32 [4096], P('col'), may hold values from 0.05 to 2
- row_output: float32 [4096], P('row'), may hold values from 0.05 to 18
- col_output: float32 [4608], P('col'), may hold values from 0.05 to 2
Outputs:
- update_query: bfloat16 [4608, 4096], P('row', 'col')
- update_output: bfloat16 [4096, 4608], P('row', 'col')
- new_row_query: float32 [4608], P('row')
- new_col_query: float32 [4096], P('col')
- new_row_output: float32 [4096], P('row')
- new_col_output: float32 [4608], P('col')
All inputs are finite; a program needn't handle non-finite values.
Results may differ from a plain program's by a relative error of at most 0.028.
Values may be sent and summed in bfloat16 or wider, within the bound.
No kernel may reach another device: no remote copies, remote signals or barrier semaphores. Data moves between devices by JAX's collectives and lax.ppermute only.
A program may use at most 128 MiB of HBM per device.

v0:
```python
import functools

import jax
import jax.numpy as jnp
from jax import lax
from jax.experimental import pallas as pl
from jax.experimental.pallas import tpu as pltpu
from jax.sharding import Mesh
from jax.sharding import PartitionSpec as P


CLIP = 3072
Y, Z, CORE, X = "row_0", "row_1", "row_2", "col"
ROW = (Y, Z, CORE)

QUERY_GRANT, OUTPUT_GRANT = 16, 16
decay_rate = 0.81
epsilon_one = 1e-30


def shift(value, axis, by):
    size = lax.axis_size(axis)
    return lax.ppermute(value, axis, [(i, (i + by) % size) for i in range(size)])


def fetch_slab(left_ref, left_buf, in_sem, runs, slot):
    at = 0
    for start, columns in runs:
        pltpu.make_async_copy(
            left_ref.at[:, pl.ds(pl.multiple_of(start, 128), columns)],
            left_buf.at[slot, :, pl.ds(at, columns)],
            in_sem.at[slot],
        ).start()
        at += columns


def slab_product(left_buf, right_ref, in_sem, slot):
    whole = left_buf.at[slot]
    pltpu.make_async_copy(whole, whole, in_sem.at[slot]).wait()
    product = lax.dot_general(
        left_buf[slot], right_ref[...], (((0,), (0,)), ((), ())), preferred_element_type=jnp.float32
    )
    return product.astype(jnp.bfloat16)


def query_kernel(
    blocks, group, where_ref, left_ref, right_ref, keep_ref, give_ref, left_buf, in_sem, out_buf
):
    core = where_ref[0]
    slots, _, width = left_buf.shape
    pieces = 8 * group // width
    slabs = [(where_ref[1 + k] + s * width) for k in blocks for s in range(pieces)]

    def fetch(i):
        fetch_slab(left_ref, left_buf, in_sem, [(slabs[i], width)], i % slots)

    for i in range(min(slots, len(slabs))):
        fetch(i)
    for b in range(len(blocks)):

        def slab_step(s, carry, b=b):
            i = b * pieces + s
            product = slab_product(left_buf, right_ref, in_sem, lax.rem(i, slots))
            out_buf[pl.ds(pl.multiple_of(s * width, 128), width), :] = product
            for j in range(slots, len(slabs)):

                @pl.when(i + slots == j)
                def _(j=j):
                    fetch(j)

            return carry

        lax.fori_loop(0, pieces, slab_step, 0)

        def split_step(e, carry, b=b):
            entry = where_ref[9 + e]
            mine = pl.multiple_of((2 * entry + core) * group, 16)
            other = pl.multiple_of((2 * entry + 1 - core) * group, 16)
            keep_ref[b, e] = out_buf[pl.ds(mine, group), :]
            give_ref[b, e] = out_buf[pl.ds(other, group), :]
            return carry

        lax.fori_loop(0, 4, split_step, 0)


def output_kernel(
    blocks, group, where_ref, left_ref, right_ref, keep_ref, give_ref, left_buf, in_sem
):
    core = where_ref[0]
    slots = left_buf.shape[0]
    slabs = [
        [(where_ref[13 + e] * (8 * group) + where_ref[5 + k] + half * group, group) for e in range(4)]
        for k in blocks
        for half in (1 - core, core)
    ]
    for i in range(min(slots, len(slabs))):
        fetch_slab(left_ref, left_buf, in_sem, slabs[i], i % slots)
    for i in range(len(slabs)):
        product = slab_product(left_buf, right_ref, in_sem, i % slots)
        target = keep_ref if i % 2 else give_ref
        target[i // 2] = product.reshape(4, group, product.shape[-1])
        if i + slots < len(slabs):
            fetch_slab(left_ref, left_buf, in_sem, slabs[i + slots], i % slots)


def partial_blocks(where, left, right, blocks, group, aligned, vmem):
    tokens, columns = right.shape
    shape = jax.ShapeDtypeStruct((len(blocks), 4, group, columns), jnp.bfloat16)
    rows = 8 * group
    width = rows // 2 if aligned else rows // 3
    scratch = [pltpu.VMEM((3, tokens, width), jnp.bfloat16), pltpu.SemaphoreType.DMA((3,))]
    if not aligned:
        scratch.append(pltpu.VMEM((rows, columns), jnp.bfloat16))
    return pl.pallas_call(
        functools.partial(output_kernel if aligned else query_kernel, blocks, group),
        out_shape=[shape, shape],
        in_specs=[
            pl.BlockSpec(memory_space=pltpu.SMEM),
            pl.BlockSpec(memory_space=pl.ANY),
            pl.BlockSpec(memory_space=pltpu.VMEM),
        ],
        out_specs=[pl.BlockSpec(memory_space=pltpu.VMEM)] * 2,
        scratch_shapes=scratch,
        compiler_params=pltpu.CompilerParams(vmem_limit_bytes=vmem * 2**20),
        cost_estimate=pl.CostEstimate(
            flops=2 * len(blocks) * rows * tokens * columns,
            bytes_accessed=2 * len(blocks) * rows * tokens,
            transcendentals=0,
        ),
    )(where, left, right)


def add_kernel(plan, step, *refs):
    inputs, outputs = refs[: len(refs) - len(plan)], refs[len(refs) - len(plan) :]
    rows = outputs[0].shape[1]
    for o, entries in enumerate(plan):
        for e, terms in enumerate(entries):

            def chunk(i, carry, o=o, e=e, terms=terms):
                at = pl.ds(pl.multiple_of(i * step, step), step)
                value = None
                for which, entry in terms:
                    term = inputs[which][entry, at, :].astype(jnp.float32)
                    value = term if value is None else value + term
                outputs[o][e, at, :] = value.astype(outputs[o].dtype)
                return carry

            lax.fori_loop(0, rows // step, chunk, 0)


def add_entries(inputs, plan, dtypes=None):
    rows, columns = inputs[0].shape[1:]
    dtypes = dtypes or [jnp.bfloat16] * len(plan)
    return pl.pallas_call(
        functools.partial(add_kernel, plan, 16),
        out_shape=[jax.ShapeDtypeStruct((len(p), rows, columns), d) for p, d in zip(plan, dtypes)],
        in_specs=[pl.BlockSpec(memory_space=pltpu.VMEM)] * len(inputs),
        out_specs=[pl.BlockSpec(memory_space=pltpu.VMEM)] * len(plan),
        cost_estimate=pl.CostEstimate(flops=600_000_000, bytes_accessed=0, transcendentals=0),
        compiler_params=pltpu.CompilerParams(vmem_limit_bytes=12 * 2**20),
    )(*inputs)


def wide(value):
    return value.astype(jnp.float32)


def after(value, *others):
    return lax.optimization_barrier((value, *others))[0]


def flat(value):
    return value.reshape(-1, *value.shape[2:])


def all_sum(value, axis):
    size = lax.axis_size(axis)
    total = value
    for k in range(1, size):
        total = total + shift(value, axis, k)
    return total


def finish(
    gradient, clip_scale, row_old, col_old, row_sums, col_sums, row_level, whole_rows, whole_cols
):
    squared_scale = clip_scale * clip_scale
    row_new = decay_rate * row_old + (1.0 - decay_rate) * (
        squared_scale * row_sums / whole_cols + epsilon_one
    )
    col_new = decay_rate * col_old + (1.0 - decay_rate) * (
        squared_scale * col_sums / whole_rows + epsilon_one
    )
    update = clip_scale * gradient * lax.rsqrt(row_new[:, None] * col_new[None, :] / row_level)
    return (update.astype(jnp.bfloat16), row_new, col_new)


def shards(acts_in, grad_query, attn_out, grad_out, row_query, col_query, row_output, col_output):
    query_rows = row_query.shape[0]
    output_rows = row_output.shape[0]
    query_width = col_query.shape[0]
    output_width = col_output.shape[0]
    y, z, core = lax.axis_index(Y), lax.axis_index(Z), lax.axis_index(CORE)
    pair_query, pair_output = 2 * query_rows, 2 * output_rows
    where = jnp.stack(
        [core]
        + [lax.rem(y + k, 4) * (4 * pair_query) for k in range(4)]
        + [lax.rem(z + k, 4) * pair_output for k in range(4)]
        + [lax.rem(z + k, 4) for k in range(4)]
        + [lax.rem(y + k, 4) for k in range(4)]
    ).astype(jnp.int32)

    def query_blocks(where, ks, vmem):
        kept, give = partial_blocks(where, acts_in, grad_query, ks, query_rows, False, vmem)
        return kept, flat(kept), flat(shift(give, CORE, 1))

    def output_blocks(where, ks, vmem):
        kept, give = partial_blocks(where, attn_out, grad_out, ks, output_rows, True, vmem)
        return kept, flat(kept), flat(shift(give, CORE, 1))

    one, two = (2, 1), (3, 0)
    far_plan = [[[(0, e), (1, e)] for e in half] for half in (one, two)]

    def near_plan(half, relayed, first, third, arrived):
        plan = [[[(i, base + e) for i in which] for e in half] for which, base in (first, third)]
        return [
            [terms + [(arrived, i)] if o == relayed else terms for i, terms in enumerate(entries)]
            for o, entries in enumerate(plan)
        ]

    query_places = (((0, 1), 0), ((0, 1), 4), 2)
    output_places = (((0, 1), 0), ((2, 3), 0), 4)
    last_one = [[[(0, e), (1, e), (2, i), (3, i)]] for i, e in enumerate(one)]
    last_two = [[[(0, e), (1, e), (2, i), (3, i)]] for i, e in enumerate(two)]

    query_made, *query_block = query_blocks(where, (2,), 50)
    output_made, *output_block = output_blocks(after(where, query_made), (2,), 44)
    query_far_one, query_far_two = add_entries(query_block, far_plan)
    query_low = shift(query_far_one, Y, 1)
    query_high = shift(query_far_two, Y, -1)
    output_far_one, output_far_two = add_entries(output_block, far_plan)
    output_low = shift(output_far_one, Z, 1)
    output_high = shift(output_far_two, Z, -1)

    ready = after(where, query_far_one, output_far_one)
    query_made, query_kept, query_got = query_blocks(ready, (1, 3), QUERY_GRANT)
    output_made, *output_1 = output_blocks(after(where, query_made), (1,), OUTPUT_GRANT)
    query_plus_one, query_minus_one = add_entries(
        (query_kept, query_got, query_low), near_plan(one, 0, *query_places)
    )
    query_one = (shift(query_plus_one, Y, 1), shift(query_minus_one, Y, -1))
    output_made, *output_3 = output_blocks(
        after(where, query_plus_one, output_made), (3,), OUTPUT_GRANT
    )
    query_plus_two, query_minus_two = add_entries(
        (query_kept, query_got, query_high), near_plan(two, 1, *query_places)
    )
    query_two = (shift(query_plus_two, Y, 1), shift(query_minus_two, Y, -1))
    output_plus_one, output_minus_one = add_entries(
        (*output_1, *output_3, output_low), near_plan(one, 0, *output_places)
    )
    output_one = (shift(output_plus_one, Z, 1), shift(output_minus_one, Z, -1))
    output_plus_two, output_minus_two = add_entries(
        (*output_1, *output_3, output_high), near_plan(two, 1, *output_places)
    )
    output_two = (shift(output_plus_two, Z, 1), shift(output_minus_two, Z, -1))

    ready = after(where, query_plus_two, output_plus_two)
    query_made, *query_block = query_blocks(ready, (0,), QUERY_GRANT)
    output_made, *output_block = output_blocks(after(where, query_made), (0,), OUTPUT_GRANT)
    wide_own = [jnp.bfloat16, jnp.float32]
    query_2, query_1 = add_entries((*query_block, *query_one), last_one)
    query_sent = [shift(query_2, Z, 2), shift(query_1, Z, 1)]
    output_2, output_1 = add_entries((*output_block, *output_one), last_one)
    output_sent = [shift(output_2, Y, 2), shift(output_1, Y, 1)]
    query_3, query_own = add_entries((*query_block, *query_two), last_two, wide_own)
    query_sent.append(shift(query_3, Z, 3))
    output_3, output_own = add_entries((*output_block, *output_two), last_two, wide_own)
    output_sent.append(shift(output_3, Y, 3))
    query_grad = query_own[0] + sum(wide(p[0]) for p in query_sent)
    output_grad = output_own[0] + sum(wide(p[0]) for p in output_sent)

    query_whole_rows = query_rows * lax.axis_size(ROW)
    output_whole_rows = output_rows * lax.axis_size(ROW)
    query_whole_cols = query_width * lax.axis_size(X)
    output_whole_cols = output_width * lax.axis_size(X)
    query_square = query_grad * query_grad
    output_square = output_grad * output_grad
    query_rowsum = jnp.sum(query_square, axis=1)
    output_rowsum = jnp.sum(output_square, axis=1)
    query_colsum = jnp.sum(query_square, axis=0)
    output_colsum = jnp.sum(output_square, axis=0)
    rowsums = all_sum(jnp.concatenate([query_rowsum, output_rowsum]), X)
    query_rowsum, output_rowsum = rowsums[:query_rows], rowsums[query_rows:]
    scalars = jnp.stack(
        [jnp.sum(query_rowsum), jnp.sum(output_rowsum), jnp.sum(row_query), jnp.sum(row_output)]
    )
    sums = jnp.concatenate([query_colsum, output_colsum, scalars])
    sums = jnp.sum(
        lax.all_to_all(
            jnp.broadcast_to(sums[None, None], (lax.axis_size(ROW), 1, sums.shape[0])),
            ROW,
            0,
            0,
            tiled=True,
        ),
        axis=(0, 1),
    )
    query_colsum = sums[:query_width]
    output_colsum = sums[query_width : query_width + output_width]
    query_squares, output_squares, query_oldsum, output_oldsum = (
        sums[query_width + output_width + i] for i in range(4)
    )
    clip_scale = CLIP / jnp.maximum(jnp.sqrt(query_squares + output_squares), jnp.float32(CLIP))
    squared_scale = clip_scale * clip_scale
    query_level = decay_rate * query_oldsum / query_whole_rows + (1.0 - decay_rate) * (
        squared_scale * query_squares / (query_whole_rows * query_whole_cols) + epsilon_one
    )
    output_level = decay_rate * output_oldsum / output_whole_rows + (1.0 - decay_rate) * (
        squared_scale * output_squares / (output_whole_rows * output_whole_cols) + epsilon_one
    )
    update_query, new_row_query, new_col_query = finish(
        query_grad,
        clip_scale,
        row_query,
        col_query,
        query_rowsum,
        query_colsum,
        query_level,
        query_whole_rows,
        query_whole_cols,
    )
    update_output, new_row_output, new_col_output = finish(
        output_grad,
        clip_scale,
        row_output,
        col_output,
        output_rowsum,
        output_colsum,
        output_level,
        output_whole_rows,
        output_whole_cols,
    )
    return (
        update_query,
        update_output,
        new_row_query,
        new_col_query,
        new_row_output,
        new_col_output,
    )


def solution(mesh):
    split = Mesh(
        mesh.devices.reshape(4, 4, 2, mesh.shape[X]), (Y, Z, CORE, X)
    )
    return jax.shard_map(
        shards,
        mesh=split,
        in_specs=(
            P(ROW, None),
            P(ROW, X),
            P(ROW, None),
            P(ROW, X),
            P(ROW),
            P(X),
            P(ROW),
            P(X),
        ),
        out_specs=(P(ROW, X), P(ROW, X), P(ROW), P(X), P(ROW), P(X)),
        check_vma=False,
    )
```

profile of v0, /device:TPU:1, one launch (start us, length us, event | category | flops | bytes accessed | tf_op | source)
XLA Modules:
  0.0 179.3 jit_solution(7674201420758167084)
XLA Ops:
  0.8 6.9 %shard_map.127 = (bf16[1,4,144,1024]{3,2,1,0:T(8,128)(2,1)S(1)}, bf16[1,4,144,1024]{3,2,1,0:T(8,128)(2,1)S(1)}) custom-call(s32[17]{0:T(128)S(1)} %stack.83.where_ref, bf16[1024,4608]{1,0:T(8,128)(2,1)} %left_ref.12, bf16[1024,1024]{1,0:T(8,128)(2,1)} %right_ref.12), custom_call_target="tpu_custom_call" | custom-call | flops 2415919104 | bytes 2359296 | tf_op jit(solution)/shard_map/pallas_call | solution.py:114
  9.1 5.7 %shard_map.129 = (bf16[1,4,128,1152]{3,2,1,0:T(8,128)(2,1)S(1)}, bf16[1,4,128,1152]{3,2,1,0:T(8,128)(2,1)S(1)}) custom-call(s32[17]{0:T(128)S(1)} %stack.83.where_ref, bf16[1024,4096]{1,0:T(8,128)(2,1)} %left_ref.13, bf16[1024,1152]{1,0:T(8,128)(2,1)S(1)} %copy-done), custom_call_target="tpu_custom_call" | custom-call | flops 2415919104 | bytes 2097152 | tf_op jit(solution)/shard_map/pallas_call | solution.py:114
  15.5 2.3 %collective-permute-done.1 = bf16[1,4,128,1152]{3,2,1,0:T(8,128)(2,1)S(1)} collective-permute-done((bf16[1,4,128,1152]{3,2,1,0:T(8,128)(2,1)S(1)}, bf16[1,4,128,1152]{3,2,1,0:T(8,128)(2,1)S(1)}, u32[]{:S(2)}, u32[]{:S(2)}) %collective-permute-start.1) | collective-permute-done | bytes 1179680 | tf_op jit(solution)/shard_map/ppermute | solution.py:23
  19.4 7.6 %shard_map.131 = (bf16[2,4,144,1024]{3,2,1,0:T(8,128)(2,1)S(1)}, bf16[2,4,144,1024]{3,2,1,0:T(8,128)(2,1)S(1)}) custom-call(s32[17]{0:T(128)S(1)} %stack.83.where_ref, bf16[1024,4608]{1,0:T(8,128)(2,1)S(1)} %bitcast.50, bf16[1024,1024]{1,0:T(8,128)(2,1)S(1)} %copy-done.1), custom_call_target="tpu_custom_call" | custom-call | flops 4831838208 | bytes 4718592 | tf_op jit(solution)/shard_map/pallas_call | solution.py:114
  28.6 4.9 %shard_map.133 = (bf16[1,4,128,1152]{3,2,1,0:T(8,128)(2,1)S(1)}, bf16[1,4,128,1152]{3,2,1,0:T(8,128)(2,1)S(1)}) custom-call(s32[17]{0:T(128)S(1)} %stack.83.where_ref, bf16[1024,4096]{1,0:T(8,128)(2,1)S(1)} %bitcast.48, bf16[1024,1152]{1,0:T(8,128)(2,1)S(1)} %copy-done), custom_call_target="tpu_custom_call" | custom-call | flops 2415919104 | bytes 2097152 | tf_op jit(solution)/shard_map/pallas_call | solution.py:114
  34.4 8.9 %collective-permute-done.5.refs_2_ = bf16[2,144,1024]{2,1,0:T(8,128)(2,1)S(1)} collective-permute-done((bf16[2,144,1024]{2,1,0:T(8,128)(2,1)S(1)}, bf16[2,144,1024]{2,1,0:T(8,128)(2,1)S(1)}, u32[]{:S(2)}, u32[]{:S(2)}) %collective-permute-start.5) | collective-permute-done | bytes 589856 | tf_op jit(solution)/shard_map/ppermute | solution.py:23
  43.8 4.9 %shard_map.135 = (bf16[1,4,128,1152]{3,2,1,0:T(8,128)(2,1)S(1)}, bf16[1,4,128,1152]{3,2,1,0:T(8,128)(2,1)S(1)}) custom-call(s32[17]{0:T(128)S(1)} %stack.83.where_ref, bf16[1024,4096]{1,0:T(8,128)(2,1)S(1)} %bitcast.48, bf16[1024,1152]{1,0:T(8,128)(2,1)S(1)} %copy-done), custom_call_target="tpu_custom_call" | custom-call | flops 2415919104 | bytes 2097152 | tf_op jit(solution)/shard_map/pallas_call | solution.py:114
  51.3 3.8 %collective-permute-start.7 = (bf16[2,128,1152]{2,1,0:T(8,128)(2,1)S(1)}, bf16[2,128,1152]{2,1,0:T(8,128)(2,1)S(1)}, u32[]{:S(2)}, u32[]{:S(2)}) collective-permute-start(bf16[2,128,1152]{2,1,0:T(8,128)(2,1)S(1)} %get-tuple-element.65), channel_id=1, source_target_pairs={{0,24},{8,0},{16,8},{24,16},{1,25},{9,1},{17,9},{25,17},{2,26},{10... | collective-permute-start | bytes 1769480 | tf_op jit(solution)/shard_map/ppermute | solution.py:23
  55.1 9.6 %collective-permute-done.3.refs_2_ = bf16[2,144,1024]{2,1,0:T(8,128)(2,1)S(1)} collective-permute-done((bf16[2,144,1024]{2,1,0:T(8,128)(2,1)S(1)}, bf16[2,144,1024]{2,1,0:T(8,128)(2,1)S(1)}, u32[]{:S(2)}, u32[]{:S(2)}) %collective-permute-start.3) | collective-permute-done | bytes 589856 | tf_op jit(solution)/shard_map/ppermute | solution.py:23
  64.6 2.7 %collective-permute-start.12 = (bf16[2,144,1024]{2,1,0:T(8,128)(2,1)S(1)}, bf16[2,144,1024]{2,1,0:T(8,128)(2,1)S(1)}, u32[]{:S(2)}, u32[]{:S(2)}) collective-permute-start(bf16[2,144,1024]{2,1,0:T(8,128)(2,1)S(1)} %get-tuple-element.72), channel_id=1, source_target_pairs={{0,96},{32,0},{64,32},{96,64},{1,97},{33,1},{65,33},{97,65},{2,98}... | collective-permute-start | bytes 1769480 | tf_op jit(solution)/shard_map/ppermute | solution.py:23
  68.5 4.0 %shard_map.137 = (bf16[1,4,144,1024]{3,2,1,0:T(8,128)(2,1)S(1)}, bf16[1,4,144,1024]{3,2,1,0:T(8,128)(2,1)S(1)}) custom-call(s32[17]{0:T(128)S(1)} %stack.83.where_ref, bf16[1024,4608]{1,0:T(8,128)(2,1)S(1)} %bitcast.50, bf16[1024,1024]{1,0:T(8,128)(2,1)S(1)} %copy-done.1), custom_call_target="tpu_custom_call" | custom-call | flops 2415919104 | bytes 2359296 | tf_op jit(solution)/shard_map/pallas_call | solution.py:114
  73.8 2.7 %collective-permute-start.10 = (bf16[2,144,1024]{2,1,0:T(8,128)(2,1)S(1)}, bf16[2,144,1024]{2,1,0:T(8,128)(2,1)S(1)}, u32[]{:S(2)}, u32[]{:S(2)}) collective-permute-start(bf16[2,144,1024]{2,1,0:T(8,128)(2,1)S(1)} %get-tuple-element.70), channel_id=1, source_target_pairs={{0,96},{32,0},{64,32},{96,64},{1,97},{33,1},{65,33},{97,65},{2,98}... | collective-permute-start | bytes 1769480 | tf_op jit(solution)/shard_map/ppermute | solution.py:23
  76.5 4.9 %shard_map.140 = (bf16[1,4,128,1152]{3,2,1,0:T(8,128)(2,1)S(1)}, bf16[1,4,128,1152]{3,2,1,0:T(8,128)(2,1)S(1)}) custom-call(s32[17]{0:T(128)S(1)} %stack.83.where_ref, bf16[1024,4096]{1,0:T(8,128)(2,1)S(1)} %bitcast.48, bf16[1024,1152]{1,0:T(8,128)(2,1)S(1)} %copy-done), custom_call_target="tpu_custom_call" | custom-call | flops 2415919104 | bytes 2097152 | tf_op jit(solution)/shard_map/pallas_call | solution.py:114
  82.6 7.2 %collective-permute-done.11.refs_2_ = bf16[2,144,1024]{2,1,0:T(8,128)(2,1)S(1)} collective-permute-done((bf16[2,144,1024]{2,1,0:T(8,128)(2,1)S(1)}, bf16[2,144,1024]{2,1,0:T(8,128)(2,1)S(1)}, u32[]{:S(2)}, u32[]{:S(2)}) %collective-permute-start.11) | collective-permute-done | bytes 589856 | tf_op jit(solution)/shard_map/ppermute | solution.py:23
  91.7 3.8 %collective-permute-start.21 = (bf16[2,128,1152]{2,1,0:T(8,128)(2,1)S(1)}, bf16[2,128,1152]{2,1,0:T(8,128)(2,1)S(1)}, u32[]{:S(2)}, u32[]{:S(2)}) collective-permute-start(bf16[2,128,1152]{2,1,0:T(8,128)(2,1)S(1)} %get-tuple-element.82), channel_id=1, source_target_pairs={{0,24},{8,0},{16,8},{24,16},{1,25},{9,1},{17,9},{25,17},{2,26},{10... | collective-permute-start | bytes 1769480 | tf_op jit(solution)/shard_map/ppermute | solution.py:23
  95.5 7.0 %collective-permute-done.9.refs_2_ = bf16[2,144,1024]{2,1,0:T(8,128)(2,1)S(1)} collective-permute-done((bf16[2,144,1024]{2,1,0:T(8,128)(2,1)S(1)}, bf16[2,144,1024]{2,1,0:T(8,128)(2,1)S(1)}, u32[]{:S(2)}, u32[]{:S(2)}) %collective-permute-start.9) | collective-permute-done | bytes 589856 | tf_op jit(solution)/shard_map/ppermute | solution.py:23
  102.5 3.8 %collective-permute-start.18 = (bf16[2,128,1152]{2,1,0:T(8,128)(2,1)S(1)}, bf16[2,128,1152]{2,1,0:T(8,128)(2,1)S(1)}, u32[]{:S(2)}, u32[]{:S(2)}) collective-permute-start(bf16[2,128,1152]{2,1,0:T(8,128)(2,1)S(1)} %get-tuple-element.79), channel_id=1, source_target_pairs={{0,24},{8,0},{16,8},{24,16},{1,25},{9,1},{17,9},{25,17},{2,26},{10... | collective-permute-start | bytes 1769480 | tf_op jit(solution)/shard_map/ppermute | solution.py:23
  108.6 2.0 %collective-permute-start.14 = (bf16[1,144,1024]{2,1,0:T(8,128)(2,1)S(1)}, bf16[1,144,1024]{2,1,0:T(8,128)(2,1)S(1)}, u32[]{:S(2)}, u32[]{:S(2)}) collective-permute-start(bf16[1,144,1024]{2,1,0:T(8,128)(2,1)S(1)} %get-tuple-element.74), channel_id=1, source_target_pairs={{0,8},{8,16},{16,24},{24,0},{1,9},{9,17},{17,25},{25,1},{2,10},{10... | collective-permute-start | bytes 884744 | tf_op jit(solution)/shard_map/ppermute | solution.py:23
  111.8 12.0 %collective-permute-done.18.refs_3_ = bf16[2,128,1152]{2,1,0:T(8,128)(2,1)S(1)} collective-permute-done((bf16[2,128,1152]{2,1,0:T(8,128)(2,1)S(1)}, bf16[2,128,1152]{2,1,0:T(8,128)(2,1)S(1)}, u32[]{:S(2)}, u32[]{:S(2)}) %collective-permute-start.18) | collective-permute-done | bytes 589856 | tf_op jit(solution)/shard_map/ppermute | solution.py:23
  127.0 6.8 %collective-permute-done.14 = bf16[1,144,1024]{2,1,0:T(8,128)(2,1)S(1)} collective-permute-done((bf16[1,144,1024]{2,1,0:T(8,128)(2,1)S(1)}, bf16[1,144,1024]{2,1,0:T(8,128)(2,1)S(1)}, u32[]{:S(2)}, u32[]{:S(2)}) %collective-permute-start.14) | collective-permute-done | bytes 294944 | tf_op jit(solution)/shard_map/ppermute | solution.py:23
  134.5 2.8 %collective-permute-start.26 = (f32[272]{0:T(512)S(1)}, f32[272]{0:T(512)S(1)}, u32[]{:S(2)}, u32[]{:S(2)}) collective-permute-start(f32[272]{0:T(512)S(1)} %pad_maximum_fusion), channel_id=1, source_target_pairs={{0,2},{1,3},{2,0},{3,1},{4,6},{5,7},{6,4},{7,5},{8,10},{9,11},{10,... | collective-permute-start | bytes 3272 | tf_op jit(solution)/shard_map/ppermute | solution.py:23
  140.0 1.8 collective-permute-done.25
  143.1 2.7 %concatenate.7 = f32[2180]{0:T(1024)S(1)} concatenate(f32[1024]{0:T(1024)S(1)} %get-tuple-element.87, f32[1152]{0:T(1024)S(1)} %get-tuple-element.89, f32[1]{0:T(128)} %bitcast.31, f32[1]{0:T(128)} %bitcast.32, f32[1]{0:T(128)} %bitcast.33, f32[1]{0:T(128)} %bitcast.34), dimensions={0} | concatenate | bytes 17440 | tf_op jit(solution)/shard_map/concatenate | solution.py:298
  145.9 26.5 %all_to_all.5 = f32[32,1,2180]{2,1,0:T(1,128)S(1)} all-to-all(f32[32,1,2180]{2,1,0:T(1,128)S(1)} %broadcast_in_dim.2), channel_id=1, replica_groups=mesh['row_0'=4,'row_1'=4,'row_2'=2,'col'=4] {'row_0','row_1','row_2'}, dimensions={0} | all-to-all | bytes 558080 | tf_op jit(solution)/shard_map/all_to_all | solution.py:300
  (101 shorter events, 29.2 us)
Async XLA Ops:
  7.7 7.3 %collective-permute-start = (bf16[1,4,144,1024]{3,2,1,0:T(8,128)(2,1)S(1)}, bf16[1,4,144,1024]{3,2,1,0:T(8,128)(2,1)S(1)}, u32[]{:S(2)}, u32[]{:S(2)}) collective-permute-start(bf16[1,4,144,1024]{3,2,1,0:T(8,128)(2,1)S(1)} %get-tuple-element.47), channel_id=1, source_target_pairs={{0,4},{4,0},{1,5},{5,1},{2,6},{6,2},{3,7},{7,3},{8,12},{12,8},{9,1... | collective-permute-start | bytes 3538952 | tf_op jit(solution)/shard_map/ppermute | solution.py:23
  27.0 16.3 %collective-permute-start.2 = (bf16[2,4,144,1024]{3,2,1,0:T(8,128)(2,1)S(1)}, bf16[2,4,144,1024]{3,2,1,0:T(8,128)(2,1)S(1)}, u32[]{:S(2)}, u32[]{:S(2)}) collective-permute-start(bf16[2,4,144,1024]{3,2,1,0:T(8,128)(2,1)S(1)} %get-tuple-element.55), channel_id=1, source_target_pairs={{0,4},{4,0},{1,5},{5,1},{2,6},{6,2},{3,7},{7,3},{8,12},{12,8},{9,1... | collective-permute-start | bytes 7077896 | tf_op jit(solution)/shard_map/ppermute | solution.py:23
  27.2 16.1 %collective-permute-start.5 = (bf16[2,144,1024]{2,1,0:T(8,128)(2,1)S(1)}, bf16[2,144,1024]{2,1,0:T(8,128)(2,1)S(1)}, u32[]{:S(2)}, u32[]{:S(2)}) collective-permute-start(bf16[2,144,1024]{2,1,0:T(8,128)(2,1)S(1)} %get-tuple-element.48), channel_id=1, source_target_pairs={{0,32},{32,64},{64,96},{96,0},{1,33},{33,65},{65,97},{97,1},{2,34}... | collective-permute-start | bytes 1769480 | tf_op jit(solution)/shard_map/ppermute | solution.py:23
  33.5 34.4 %collective-permute-start.4 = (bf16[1,4,128,1152]{3,2,1,0:T(8,128)(2,1)S(1)}, bf16[1,4,128,1152]{3,2,1,0:T(8,128)(2,1)S(1)}, u32[]{:S(2)}, u32[]{:S(2)}) collective-permute-start(bf16[1,4,128,1152]{3,2,1,0:T(8,128)(2,1)S(1)} %get-tuple-element.60), channel_id=1, source_target_pairs={{0,4},{4,0},{1,5},{5,1},{2,6},{6,2},{3,7},{7,3},{8,12},{12,8},{9,1... | collective-permute-start | bytes 3538952 | tf_op jit(solution)/shard_map/ppermute | solution.py:23
  48.7 19.2 %collective-permute-start.6 = (bf16[1,4,128,1152]{3,2,1,0:T(8,128)(2,1)S(1)}, bf16[1,4,128,1152]{3,2,1,0:T(8,128)(2,1)S(1)}, u32[]{:S(2)}, u32[]{:S(2)}) collective-permute-start(bf16[1,4,128,1152]{3,2,1,0:T(8,128)(2,1)S(1)} %get-tuple-element.64), channel_id=1, source_target_pairs={{0,4},{4,0},{1,5},{5,1},{2,6},{6,2},{3,7},{7,3},{8,12},{12,8},{9,1... | collective-permute-start | bytes 3538952 | tf_op jit(solution)/shard_map/ppermute | solution.py:23
  49.8 14.8 %collective-permute-start.3 = (bf16[2,144,1024]{2,1,0:T(8,128)(2,1)S(1)}, bf16[2,144,1024]{2,1,0:T(8,128)(2,1)S(1)}, u32[]{:S(2)}, u32[]{:S(2)}) collective-permute-start(bf16[2,144,1024]{2,1,0:T(8,128)(2,1)S(1)} %get-tuple-element.56), channel_id=1, source_target_pairs={{0,96},{32,0},{64,32},{96,64},{1,97},{33,1},{65,33},{97,65},{2,98}... | collective-permute-start | bytes 1769480 | tf_op jit(solution)/shard_map/ppermute | solution.py:23
  51.3 16.6 %collective-permute-start.7 = (bf16[2,128,1152]{2,1,0:T(8,128)(2,1)S(1)}, bf16[2,128,1152]{2,1,0:T(8,128)(2,1)S(1)}, u32[]{:S(2)}, u32[]{:S(2)}) collective-permute-start(bf16[2,128,1152]{2,1,0:T(8,128)(2,1)S(1)} %get-tuple-element.65), channel_id=1, source_target_pairs={{0,24},{8,0},{16,8},{24,16},{1,25},{9,1},{17,9},{25,17},{2,26},{10... | collective-permute-start | bytes 1769480 | tf_op jit(solution)/shard_map/ppermute | solution.py:23
  55.1 26.3 %collective-permute-start.19 = (bf16[2,128,1152]{2,1,0:T(8,128)(2,1)S(1)}, bf16[2,128,1152]{2,1,0:T(8,128)(2,1)S(1)}, u32[]{:S(2)}, u32[]{:S(2)}) collective-permute-start(bf16[2,128,1152]{2,1,0:T(8,128)(2,1)S(1)} %get-tuple-element.52), channel_id=1, source_target_pairs={{0,8},{8,16},{16,24},{24,0},{1,9},{9,17},{17,25},{25,1},{2,10},{10... | collective-permute-start | bytes 1769480 | tf_op jit(solution)/shard_map/ppermute | solution.py:23
  64.6 17.4 %collective-permute-start.12 = (bf16[2,144,1024]{2,1,0:T(8,128)(2,1)S(1)}, bf16[2,144,1024]{2,1,0:T(8,128)(2,1)S(1)}, u32[]{:S(2)}, u32[]{:S(2)}) collective-permute-start(bf16[2,144,1024]{2,1,0:T(8,128)(2,1)S(1)} %get-tuple-element.72), channel_id=1, source_target_pairs={{0,96},{32,0},{64,32},{96,64},{1,97},{33,1},{65,33},{97,65},{2,98}... | collective-permute-start | bytes 1769480 | tf_op jit(solution)/shard_map/ppermute | solution.py:23
  72.5 33.7 %collective-permute-start.8 = (bf16[1,4,144,1024]{3,2,1,0:T(8,128)(2,1)S(1)}, bf16[1,4,144,1024]{3,2,1,0:T(8,128)(2,1)S(1)}, u32[]{:S(2)}, u32[]{:S(2)}) collective-permute-start(bf16[1,4,144,1024]{3,2,1,0:T(8,128)(2,1)S(1)} %get-tuple-element.69), channel_id=1, source_target_pairs={{0,4},{4,0},{1,5},{5,1},{2,6},{6,2},{3,7},{7,3},{8,12},{12,8},{9,1... | collective-permute-start | bytes 3538952 | tf_op jit(solution)/shard_map/ppermute | solution.py:23
  73.8 16.0 %collective-permute-start.11 = (bf16[2,144,1024]{2,1,0:T(8,128)(2,1)S(1)}, bf16[2,144,1024]{2,1,0:T(8,128)(2,1)S(1)}, u32[]{:S(2)}, u32[]{:S(2)}) collective-permute-start(bf16[2,144,1024]{2,1,0:T(8,128)(2,1)S(1)} %get-tuple-element.61), channel_id=1, source_target_pairs={{0,32},{32,64},{64,96},{96,0},{1,33},{33,65},{65,97},{97,1},{2,34}... | collective-permute-start | bytes 1769480 | tf_op jit(solution)/shard_map/ppermute | solution.py:23
  73.8 17.9 %collective-permute-start.10 = (bf16[2,144,1024]{2,1,0:T(8,128)(2,1)S(1)}, bf16[2,144,1024]{2,1,0:T(8,128)(2,1)S(1)}, u32[]{:S(2)}, u32[]{:S(2)}) collective-permute-start(bf16[2,144,1024]{2,1,0:T(8,128)(2,1)S(1)} %get-tuple-element.70), channel_id=1, source_target_pairs={{0,96},{32,0},{64,32},{96,64},{1,97},{33,1},{65,33},{97,65},{2,98}... | collective-permute-start | bytes 1769480 | tf_op jit(solution)/shard_map/ppermute | solution.py:23
  81.4 29.3 %collective-permute-start.16 = (bf16[1,4,128,1152]{3,2,1,0:T(8,128)(2,1)S(1)}, bf16[1,4,128,1152]{3,2,1,0:T(8,128)(2,1)S(1)}, u32[]{:S(2)}, u32[]{:S(2)}) collective-permute-start(bf16[1,4,128,1152]{3,2,1,0:T(8,128)(2,1)S(1)} %get-tuple-element.78), channel_id=1, source_target_pairs={{0,4},{4,0},{1,5},{5,1},{2,6},{6,2},{3,7},{7,3},{8,12},{12,8},{9,1... | collective-permute-start | bytes 3538952 | tf_op jit(solution)/shard_map/ppermute | solution.py:23
  82.1 20.4 %collective-permute-start.9 = (bf16[2,144,1024]{2,1,0:T(8,128)(2,1)S(1)}, bf16[2,144,1024]{2,1,0:T(8,128)(2,1)S(1)}, u32[]{:S(2)}, u32[]{:S(2)}) collective-permute-start(bf16[2,144,1024]{2,1,0:T(8,128)(2,1)S(1)} %get-tuple-element.57), channel_id=1, source_target_pairs={{0,32},{32,64},{64,96},{96,0},{1,33},{33,65},{65,97},{97,1},{2,34}... | collective-permute-start | bytes 1769480 | tf_op jit(solution)/shard_map/ppermute | solution.py:23
  89.8 16.8 %collective-permute-start.20 = (bf16[2,128,1152]{2,1,0:T(8,128)(2,1)S(1)}, bf16[2,128,1152]{2,1,0:T(8,128)(2,1)S(1)}, u32[]{:S(2)}, u32[]{:S(2)}) collective-permute-start(bf16[2,128,1152]{2,1,0:T(8,128)(2,1)S(1)} %get-tuple-element.81), channel_id=1, source_target_pairs={{0,8},{8,16},{16,24},{24,0},{1,9},{9,17},{17,25},{25,1},{2,10},{10... | collective-permute-start | bytes 1769480 | tf_op jit(solution)/shard_map/ppermute | solution.py:23
  91.7 16.9 %collective-permute-start.21 = (bf16[2,128,1152]{2,1,0:T(8,128)(2,1)S(1)}, bf16[2,128,1152]{2,1,0:T(8,128)(2,1)S(1)}, u32[]{:S(2)}, u32[]{:S(2)}) collective-permute-start(bf16[2,128,1152]{2,1,0:T(8,128)(2,1)S(1)} %get-tuple-element.82), channel_id=1, source_target_pairs={{0,24},{8,0},{16,8},{24,16},{1,25},{9,1},{17,9},{25,17},{2,26},{10... | collective-permute-start | bytes 1769480 | tf_op jit(solution)/shard_map/ppermute | solution.py:23
  102.5 21.3 %collective-permute-start.18 = (bf16[2,128,1152]{2,1,0:T(8,128)(2,1)S(1)}, bf16[2,128,1152]{2,1,0:T(8,128)(2,1)S(1)}, u32[]{:S(2)}, u32[]{:S(2)}) collective-permute-start(bf16[2,128,1152]{2,1,0:T(8,128)(2,1)S(1)} %get-tuple-element.79), channel_id=1, source_target_pairs={{0,24},{8,0},{16,8},{24,16},{1,25},{9,1},{17,9},{25,17},{2,26},{10... | collective-permute-start | bytes 1769480 | tf_op jit(solution)/shard_map/ppermute | solution.py:23
  106.2 17.6 %collective-permute-start.17 = (bf16[2,128,1152]{2,1,0:T(8,128)(2,1)S(1)}, bf16[2,128,1152]{2,1,0:T(8,128)(2,1)S(1)}, u32[]{:S(2)}, u32[]{:S(2)}) collective-permute-start(bf16[2,128,1152]{2,1,0:T(8,128)(2,1)S(1)} %get-tuple-element.66), channel_id=1, source_target_pairs={{0,8},{8,16},{16,24},{24,0},{1,9},{9,17},{17,25},{25,1},{2,10},{10... | collective-permute-start | bytes 1769480 | tf_op jit(solution)/shard_map/ppermute | solution.py:23
  106.7 19.5 %collective-permute-start.13 = (bf16[1,144,1024]{2,1,0:T(8,128)(2,1)S(1)}, bf16[1,144,1024]{2,1,0:T(8,128)(2,1)S(1)}, u32[]{:S(2)}, u32[]{:S(2)}) collective-permute-start(bf16[1,144,1024]{2,1,0:T(8,128)(2,1)S(1)} %get-tuple-element.73), channel_id=1, source_target_pairs={{0,16},{8,24},{16,0},{24,8},{1,17},{9,25},{17,1},{25,9},{2,18},{10... | collective-permute-start | bytes 884744 | tf_op jit(solution)/shard_map/ppermute | solution.py:23
  108.6 25.1 %collective-permute-start.14 = (bf16[1,144,1024]{2,1,0:T(8,128)(2,1)S(1)}, bf16[1,144,1024]{2,1,0:T(8,128)(2,1)S(1)}, u32[]{:S(2)}, u32[]{:S(2)}) collective-permute-start(bf16[1,144,1024]{2,1,0:T(8,128)(2,1)S(1)} %get-tuple-element.74), channel_id=1, source_target_pairs={{0,8},{8,16},{16,24},{24,0},{1,9},{9,17},{17,25},{25,1},{2,10},{10... | collective-permute-start | bytes 884744 | tf_op jit(solution)/shard_map/ppermute | solution.py:23
  110.7 23.1 %collective-permute-start.15 = (bf16[1,144,1024]{2,1,0:T(8,128)(2,1)S(1)}, bf16[1,144,1024]{2,1,0:T(8,128)(2,1)S(1)}, u32[]{:S(2)}, u32[]{:S(2)}) collective-permute-start(bf16[1,144,1024]{2,1,0:T(8,128)(2,1)S(1)} %get-tuple-element.75), channel_id=1, source_target_pairs={{0,24},{8,0},{16,8},{24,16},{1,25},{9,1},{17,9},{25,17},{2,26},{10... | collective-permute-start | bytes 884744 | tf_op jit(solution)/shard_map/ppermute | solution.py:23
  123.8 10.3 %collective-permute-start.22 = (bf16[1,128,1152]{2,1,0:T(8,128)(2,1)S(1)}, bf16[1,128,1152]{2,1,0:T(8,128)(2,1)S(1)}, u32[]{:S(2)}, u32[]{:S(2)}) collective-permute-start(bf16[1,128,1152]{2,1,0:T(8,128)(2,1)S(1)} %get-tuple-element.83), channel_id=1, source_target_pairs={{0,64},{32,96},{64,0},{96,32},{1,65},{33,97},{65,1},{97,33},{2,66}... | collective-permute-start | bytes 884744 | tf_op jit(solution)/shard_map/ppermute | solution.py:23
  123.8 10.3 %collective-permute-start.23 = (bf16[1,128,1152]{2,1,0:T(8,128)(2,1)S(1)}, bf16[1,128,1152]{2,1,0:T(8,128)(2,1)S(1)}, u32[]{:S(2)}, u32[]{:S(2)}) collective-permute-start(bf16[1,128,1152]{2,1,0:T(8,128)(2,1)S(1)} %get-tuple-element.84), channel_id=1, source_target_pairs={{0,32},{32,64},{64,96},{96,0},{1,33},{33,65},{65,97},{97,1},{2,34}... | collective-permute-start | bytes 884744 | tf_op jit(solution)/shard_map/ppermute | solution.py:23
  126.1 8.0 %collective-permute-start.24 = (bf16[1,128,1152]{2,1,0:T(8,128)(2,1)S(1)}, bf16[1,128,1152]{2,1,0:T(8,128)(2,1)S(1)}, u32[]{:S(2)}, u32[]{:S(2)}) collective-permute-start(bf16[1,128,1152]{2,1,0:T(8,128)(2,1)S(1)} %get-tuple-element.85), channel_id=1, source_target_pairs={{0,96},{32,0},{64,32},{96,64},{1,97},{33,1},{65,33},{97,65},{2,98}... | collective-permute-start | bytes 884744 | tf_op jit(solution)/shard_map/ppermute | solution.py:23
  (19 other events, 194.6 us)
where the time goes:
time: 180 us; the launch traced here: 179 us
  waiting for transfers between devices  56.8 us (32%)
  Pallas kernels  43.5 us (24%)
  starting transfers between devices  37.4 us (21%)
  blocking collectives  26.5 us (15%)
  other arithmetic  5.23 us (3%)
  between operations  5.21 us (3%)
  local copies, waits for them, and re-layouts  4.66 us (3%)
    ppermute x28, waiting for transfers between devices, shift(): lax.ppermute(value, axis, [(i, (i + by) % size) for i in range(size)])  56.8 us
    pallas_call x7, Pallas kernels, partial_blocks(): pl.pallas_call(functools.partial(output_kernel if aligned else query_kern...  38.8 us
    ppermute x28, starting transfers between devices, shift(): lax.ppermute(value, axis, [(i, (i + by) % size) for i in range(size)])  37.4 us
    all_to_all x1, blocking collectives, shards(): lax.all_to_all(jnp.broadcast_to(sums[None, None], (lax.axis_size(ROW), 1,...  26.5 us
    pallas_call x10, Pallas kernels, add_entries(): pl.pallas_call(functools.partial(add_kernel, plan, 16), out_shape=[jax.Sh...  4.66 us
  transfers between devices with their start and end apart: 28, of which 11 were waited for; matrix products, arithmetic and copies ran while one was open for 1% of the time, Pallas kernels for 16%

commit v1 on v0

--- a/solution.py
+++ b/solution.py
@@ -13,7 +13,7 @@
 Y, Z, CORE, X = "row_0", "row_1", "row_2", "col"
 ROW = (Y, Z, CORE)
 
-QUERY_GRANT, OUTPUT_GRANT = 16, 16
+GRANTS = 50, 46, 45, 40, 42, 42
 decay_rate = 0.81
 epsilon_one = 1e-30
 
@@ -23,96 +23,61 @@
     return lax.ppermute(value, axis, [(i, (i + by) % size) for i in range(size)])
 
 
-def fetch_slab(left_ref, left_buf, in_sem, runs, slot):
-    at = 0
-    for start, columns in runs:
-        pltpu.make_async_copy(
-            left_ref.at[:, pl.ds(pl.multiple_of(start, 128), columns)],
-            left_buf.at[slot, :, pl.ds(at, columns)],
-            in_sem.at[slot],
-        ).start()
-        at += columns
-
-
-def slab_product(left_buf, right_ref, in_sem, slot):
-    whole = left_buf.at[slot]
-    pltpu.make_async_copy(whole, whole, in_sem.at[slot]).wait()
-    product = lax.dot_general(
-        left_buf[slot], right_ref[...], (((0,), (0,)), ((), ())), preferred_element_type=jnp.float32
-    )
-    return product.astype(jnp.bfloat16)
-
-
-def query_kernel(
-    blocks, group, where_ref, left_ref, right_ref, keep_ref, give_ref, left_buf, in_sem, out_buf
+def block_kernel(
+    slabs, group, where_ref, left_ref, right_ref, keep_ref, give_ref, left_buf, in_sem, out_buf, out_sem
 ):
     core = where_ref[0]
     slots, _, width = left_buf.shape
-    pieces = 8 * group // width
-    slabs = [(where_ref[1 + k] + s * width) for k in blocks for s in range(pieces)]
+    flat_slabs = [(b, s, runs) for b, (block, _) in enumerate(slabs) for s, runs in enumerate(block)]
 
     def fetch(i):
-        fetch_slab(left_ref, left_buf, in_sem, [(slabs[i], width)], i % slots)
-
-    for i in range(min(slots, len(slabs))):
+        at = 0
+        for index, plus, columns in flat_slabs[i][2]:
+            start = pl.multiple_of(where_ref[index] + plus, 128)
+            pltpu.make_async_copy(
+                left_ref.at[:, pl.ds(start, columns)],
+                left_buf.at[i % slots, :, pl.ds(at, columns)],
+                in_sem.at[i % slots],
+            ).start()
+            at += columns
+
+    for i in range(min(slots, len(flat_slabs))):
         fetch(i)
-    for b in range(len(blocks)):
-
-        def slab_step(s, carry, b=b):
-            i = b * pieces + s
-            product = slab_product(left_buf, right_ref, in_sem, lax.rem(i, slots))
-            out_buf[pl.ds(pl.multiple_of(s * width, 128), width), :] = product
-            for j in range(slots, len(slabs)):
-
-                @pl.when(i + slots == j)
-                def _(j=j):
-                    fetch(j)
-
-            return carry
-
-        lax.fori_loop(0, pieces, slab_step, 0)
-
-        def split_step(e, carry, b=b):
-            entry = where_ref[9 + e]
-            mine = pl.multiple_of((2 * entry + core) * group, 16)
-            other = pl.multiple_of((2 * entry + 1 - core) * group, 16)
-            keep_ref[b, e] = out_buf[pl.ds(mine, group), :]
-            give_ref[b, e] = out_buf[pl.ds(other, group), :]
-            return carry
-
-        lax.fori_loop(0, 4, split_step, 0)
-
-
-def output_kernel(
-    blocks, group, where_ref, left_ref, right_ref, keep_ref, give_ref, left_buf, in_sem
-):
-    core = where_ref[0]
-    slots = left_buf.shape[0]
-    slabs = [
-        [(where_ref[13 + e] * (8 * group) + where_ref[5 + k] + half * group, group) for e in range(4)]
-        for k in blocks
-        for half in (1 - core, core)
-    ]
-    for i in range(min(slots, len(slabs))):
-        fetch_slab(left_ref, left_buf, in_sem, slabs[i], i % slots)
-    for i in range(len(slabs)):
-        product = slab_product(left_buf, right_ref, in_sem, i % slots)
-        target = keep_ref if i % 2 else give_ref
-        target[i // 2] = product.reshape(4, group, product.shape[-1])
-        if i + slots < len(slabs):
-            fetch_slab(left_ref, left_buf, in_sem, slabs[i + slots], i % slots)
-
-
-def partial_blocks(where, left, right, blocks, group, aligned, vmem):
+    for i, (b, s, _) in enumerate(flat_slabs):
+        slot = i % slots
+        whole = left_buf.at[slot]
+        pltpu.make_async_copy(whole, whole, in_sem.at[slot]).wait()
+        product = lax.dot_general(
+            left_buf[slot], right_ref[...], (((0,), (0,)), ((), ())), preferred_element_type=jnp.float32
+        )
+        out_buf[b, pl.ds(s * width, width), :] = product.astype(jnp.bfloat16)
+        if i + slots < len(flat_slabs):
+            fetch(i + slots)
+        for j in range(s * width // group, (s + 1) * width // group):
+            moved(group, slabs[b][1], where_ref, core, keep_ref, give_ref, out_buf, out_sem, b, j)
+    for b in range(len(slabs)):
+        for j in range(8):
+            rows = out_buf.at[b, pl.ds(j * group, group), :]
+            pltpu.make_async_copy(rows, keep_ref.at[b, j // 2], out_sem.at[b, j]).wait()
+
+
+def moved(group, first, where_ref, core, keep_ref, give_ref, out_buf, out_sem, b, j):
+    rows = out_buf.at[b, pl.ds(j * group, group), :]
+    entry = where_ref[first + j // 2]
+    for side, target in ((True, keep_ref), (False, give_ref)):
+
+        @pl.when((core == j % 2) == side)
+        def _(target=target):
+            pltpu.make_async_copy(rows, target.at[b, entry], out_sem.at[b, j]).start()
+
+
+def partial_blocks(where, left, right, slabs, group, vmem):
     tokens, columns = right.shape
-    shape = jax.ShapeDtypeStruct((len(blocks), 4, group, columns), jnp.bfloat16)
-    rows = 8 * group
-    width = rows // 2 if aligned else rows // 3
-    scratch = [pltpu.VMEM((3, tokens, width), jnp.bfloat16), pltpu.SemaphoreType.DMA((3,))]
-    if not aligned:
-        scratch.append(pltpu.VMEM((rows, columns), jnp.bfloat16))
+    blocks, rows = len(slabs), 8 * group
+    shape = jax.ShapeDtypeStruct((blocks, 4, group, columns), jnp.bfloat16)
+    width = rows // len(slabs[0][0])
     return pl.pallas_call(
-        functools.partial(output_kernel if aligned else query_kernel, blocks, group),
+        functools.partial(block_kernel, slabs, group),
         out_shape=[shape, shape],
         in_specs=[
             pl.BlockSpec(memory_space=pltpu.SMEM),
@@ -120,11 +85,16 @@
             pl.BlockSpec(memory_space=pltpu.VMEM),
         ],
         out_specs=[pl.BlockSpec(memory_space=pltpu.VMEM)] * 2,
-        scratch_shapes=scratch,
+        scratch_shapes=[
+            pltpu.VMEM((3, tokens, width), jnp.bfloat16),
+            pltpu.SemaphoreType.DMA((3,)),
+            pltpu.VMEM((blocks, rows, columns), jnp.bfloat16),
+            pltpu.SemaphoreType.DMA((blocks, 8)),
+        ],
         compiler_params=pltpu.CompilerParams(vmem_limit_bytes=vmem * 2**20),
         cost_estimate=pl.CostEstimate(
-            flops=2 * len(blocks) * rows * tokens * columns,
-            bytes_accessed=2 * len(blocks) * rows * tokens,
+            flops=2 * blocks * rows * tokens * columns,
+            bytes_accessed=2 * blocks * rows * tokens,
             transcendentals=0,
         ),
     )(where, left, right)
@@ -206,35 +176,38 @@
         [core]
         + [lax.rem(y + k, 4) * (4 * pair_query) for k in range(4)]
         + [lax.rem(z + k, 4) * pair_output for k in range(4)]
-        + [lax.rem(z + k, 4) for k in range(4)]
-        + [lax.rem(y + k, 4) for k in range(4)]
+        + [lax.rem(k + 4 - z, 4) for k in range(4)]
+        + [lax.rem(k + 4 - y, 4) for k in range(4)]
     ).astype(jnp.int32)
 
+    def made(where, left, right, slabs, group, vmem):
+        kept, give = partial_blocks(where, left, right, slabs, group, vmem)
+        return kept, flat(kept), flat(shift(give, CORE, 1))
+
     def query_blocks(where, ks, vmem):
-        kept, give = partial_blocks(where, acts_in, grad_query, ks, query_rows, False, vmem)
-        return kept, flat(kept), flat(shift(give, CORE, 1))
+        third = 8 * query_rows // 3
+        slabs = [([[(1 + k, s * third, third)] for s in range(3)], 9) for k in ks]
+        return made(where, acts_in, grad_query, slabs, query_rows, vmem)
 
     def output_blocks(where, ks, vmem):
-        kept, give = partial_blocks(where, attn_out, grad_out, ks, output_rows, True, vmem)
-        return kept, flat(kept), flat(shift(give, CORE, 1))
+        run = lambda k, i: (5 + k, i * 4 * pair_output, pair_output)
+        slabs = [([[run(k, 0), run(k, 1)], [run(k, 2), run(k, 3)]], 13) for k in ks]
+        return made(where, attn_out, grad_out, slabs, output_rows, vmem)
 
     one, two = (2, 1), (3, 0)
     far_plan = [[[(0, e), (1, e)] for e in half] for half in (one, two)]
 
-    def near_plan(half, relayed, first, third, arrived):
-        plan = [[[(i, base + e) for i in which] for e in half] for which, base in (first, third)]
-        return [
-            [terms + [(arrived, i)] if o == relayed else terms for i, terms in enumerate(entries)]
-            for o, entries in enumerate(plan)
-        ]
-
-    query_places = (((0, 1), 0), ((0, 1), 4), 2)
-    output_places = (((0, 1), 0), ((2, 3), 0), 4)
+    def near_plan(half, relayed):
+        plan = [[[(0, base + e), (1, base + e)] for e in half] for base in (0, 4)]
+        for i, terms in enumerate(plan[relayed]):
+            terms.append((2, i))
+        return plan
+
     last_one = [[[(0, e), (1, e), (2, i), (3, i)]] for i, e in enumerate(one)]
     last_two = [[[(0, e), (1, e), (2, i), (3, i)]] for i, e in enumerate(two)]
 
-    query_made, *query_block = query_blocks(where, (2,), 50)
-    output_made, *output_block = output_blocks(after(where, query_made), (2,), 44)
+    query_made, *query_block = query_blocks(where, (2,), GRANTS[0])
+    output_made, *output_block = output_blocks(after(where, query_made), (2,), GRANTS[1])
     query_far_one, query_far_two = add_entries(query_block, far_plan)
     query_low = shift(query_far_one, Y, 1)
     query_high = shift(query_far_two, Y, -1)
@@ -243,31 +216,21 @@
     output_high = shift(output_far_two, Z, -1)
 
     ready = after(where, query_far_one, output_far_one)
-    query_made, query_kept, query_got = query_blocks(ready, (1, 3), QUERY_GRANT)
-    output_made, *output_1 = output_blocks(after(where, query_made), (1,), OUTPUT_GRANT)
-    query_plus_one, query_minus_one = add_entries(
-        (query_kept, query_got, query_low), near_plan(one, 0, *query_places)
-    )
-    query_one = (shift(query_plus_one, Y, 1), shift(query_minus_one, Y, -1))
-    output_made, *output_3 = output_blocks(
-        after(where, query_plus_one, output_made), (3,), OUTPUT_GRANT
-    )
-    query_plus_two, query_minus_two = add_entries(
-        (query_kept, query_got, query_high), near_plan(two, 1, *query_places)
-    )
-    query_two = (shift(query_plus_two, Y, 1), shift(query_minus_two, Y, -1))
-    output_plus_one, output_minus_one = add_entries(
-        (*output_1, *output_3, output_low), near_plan(one, 0, *output_places)
-    )
-    output_one = (shift(output_plus_one, Z, 1), shift(output_minus_one, Z, -1))
-    output_plus_two, output_minus_two = add_entries(
-        (*output_1, *output_3, output_high), near_plan(two, 1, *output_places)
-    )
-    output_two = (shift(output_plus_two, Z, 1), shift(output_minus_two, Z, -1))
-
-    ready = after(where, query_plus_two, output_plus_two)
-    query_made, *query_block = query_blocks(ready, (0,), QUERY_GRANT)
-    output_made, *output_block = output_blocks(after(where, query_made), (0,), OUTPUT_GRANT)
+    query_made, *query_block = query_blocks(ready, (1, 3), GRANTS[2])
+    output_made, *output_block = output_blocks(after(where, query_made), (1, 3), GRANTS[3])
+
+    def near(block, arrived, half, relayed, axis):
+        plus, minus = add_entries((*block, arrived), near_plan(half, relayed))
+        return plus, (shift(plus, axis, 1), shift(minus, axis, -1))
+
+    query_plus, query_one = near(query_block, query_low, one, 0, Y)
+    output_plus, output_one = near(output_block, output_low, one, 0, Z)
+    query_plus, query_two = near(query_block, query_high, two, 1, Y)
+    output_plus, output_two = near(output_block, output_high, two, 1, Z)
+
+    ready = after(where, query_plus, output_plus)
+    query_made, *query_block = query_blocks(ready, (0,), GRANTS[4])
+    output_made, *output_block = output_blocks(after(where, query_made), (0,), GRANTS[5])
     wide_own = [jnp.bfloat16, jnp.float32]
     query_2, query_1 = add_entries((*query_block, *query_one), last_one)
     query_sent = [shift(query_2, Z, 2), shift(query_1, Z, 1)]

time: 180 us -> 180 us (level)
  Pallas kernels: 43.5 us -> 48.9 us
  waiting for transfers between devices: 56.8 us -> 54 us
  starting transfers between devices: 37.4 us -> 35.5 us
    pallas_call x7 -> x6, Pallas kernels: 38.8 us -> 43.4 us  [partial_blocks(): pl.pallas_call(functools.partial(block_kernel, slabs, group), out_shape=[...]
    ppermute x28 -> x27, waiting for transfers between devices: 56.8 us -> 54 us  [shift(): lax.ppermute(value, axis, [(i, (i + by) % size) for i in range(size)])]
    ppermute x28 -> x27, starting transfers between devices: 37.4 us -> 35.5 us  [shift(): lax.ppermute(value, axis, [(i, (i + by) % size) for i in range(size)])]
  transfers between devices with their start and end apart: 28 -> 27, of which waited for: 11 -> 9; matrix products, arithmetic and copies ran while one was open for 1% -> 1% of each run, Pallas kernels for 16% -> 18%
where the time goes in v1:
time: 180 us
  waiting for transfers between devices  54 us (30%)
  Pallas kernels  48.9 us (27%)
  starting transfers between devices  35.5 us (20%)
  blocking collectives  26.2 us (15%)
  other arithmetic  5.24 us (3%)
  between operations  5.14 us (3%)
  local copies, waits for them, and re-layouts  4.68 us (3%)
    ppermute x27, waiting for transfers between devices, shift(): lax.ppermute(value, axis, [(i, (i + by) % size) for i in range(size)])  54 us
    pallas_call x6, Pallas kernels, partial_blocks(): pl.pallas_call(functools.partial(block_kernel, slabs, group), out_shape=[...  43.4 us
    ppermute x27, starting transfers between devices, shift(): lax.ppermute(value, axis, [(i, (i + by) % size) for i in range(size)])  35.5 us
    all_to_all x1, blocking collectives, shards(): lax.all_to_all(jnp.broadcast_to(sums[None, None], (lax.axis_size(ROW), 1,...  26.2 us
    pallas_call x10, Pallas kernels, add_entries(): pl.pallas_call(functools.partial(add_kernel, plan, 16), out_shape=[jax.Sh...  5.49 us
  transfers between devices with their start and end apart: 27, of which 9 were waited for; matrix products, arithmetic and copies ran while one was open for 1% of the time, Pallas kernels for 18%

profile of v1, /device:TPU:1, one launch (start us, length us, event | category | flops | bytes accessed | tf_op | source)
XLA Modules:
  0.0 179.7 jit_solution(6013738136072289601)
XLA Ops:
  0.8 6.5 %shard_map.127 = (bf16[1,4,144,1024]{3,2,1,0:T(8,128)(2,1)S(1)}, bf16[1,4,144,1024]{3,2,1,0:T(8,128)(2,1)S(1)}) custom-call(s32[17]{0:T(128)S(1)} %stack.83.where_ref, bf16[1024,4608]{1,0:T(8,128)(2,1)} %left_ref.10, bf16[1024,1024]{1,0:T(8,128)(2,1)} %right_ref.10), custom_call_target="tpu_custom_call" | custom-call | flops 2415919104 | bytes 2359296 | tf_op jit(solution)/shard_map/pallas_call | solution.py:79
  8.8 6.1 %shard_map.129 = (bf16[1,4,128,1152]{3,2,1,0:T(8,128)(2,1)S(1)}, bf16[1,4,128,1152]{3,2,1,0:T(8,128)(2,1)S(1)}) custom-call(s32[17]{0:T(128)S(1)} %stack.83.where_ref, bf16[1024,4096]{1,0:T(8,128)(2,1)} %left_ref.11, bf16[1024,1152]{1,0:T(8,128)(2,1)S(1)} %copy-done), custom_call_target="tpu_custom_call" | custom-call | flops 2415919104 | bytes 2097152 | tf_op jit(solution)/shard_map/pallas_call | solution.py:79
  15.4 2.3 %collective-permute-done.1 = bf16[1,4,128,1152]{3,2,1,0:T(8,128)(2,1)S(1)} collective-permute-done((bf16[1,4,128,1152]{3,2,1,0:T(8,128)(2,1)S(1)}, bf16[1,4,128,1152]{3,2,1,0:T(8,128)(2,1)S(1)}, u32[]{:S(2)}, u32[]{:S(2)}) %collective-permute-start.1) | collective-permute-done | bytes 1179680 | tf_op jit(solution)/shard_map/ppermute | solution.py:23
  19.4 9.0 %shard_map.131 = (bf16[2,4,144,1024]{3,2,1,0:T(8,128)(2,1)S(1)}, bf16[2,4,144,1024]{3,2,1,0:T(8,128)(2,1)S(1)}) custom-call(s32[17]{0:T(128)S(1)} %stack.83.where_ref, bf16[1024,4608]{1,0:T(8,128)(2,1)} %left_ref.10, bf16[1024,1024]{1,0:T(8,128)(2,1)S(1)} %copy-done.1), custom_call_target="tpu_custom_call" | custom-call | flops 4831838208 | bytes 4718592 | tf_op jit(solution)/shard_map/pallas_call | solution.py:79
  28.8 10.4 %shard_map.133 = (bf16[2,4,128,1152]{3,2,1,0:T(8,128)(2,1)S(1)}, bf16[2,4,128,1152]{3,2,1,0:T(8,128)(2,1)S(1)}) custom-call(s32[17]{0:T(128)S(1)} %stack.83.where_ref, bf16[1024,4096]{1,0:T(8,128)(2,1)} %left_ref.11, bf16[1024,1152]{1,0:T(8,128)(2,1)S(1)} %copy-done), custom_call_target="tpu_custom_call" | custom-call | flops 4831838208 | bytes 4194304 | tf_op jit(solution)/shard_map/pallas_call | solution.py:79
  42.5 3.8 %collective-permute-start.5 = (bf16[2,128,1152]{2,1,0:T(8,128)(2,1)S(1)}, bf16[2,128,1152]{2,1,0:T(8,128)(2,1)S(1)}, u32[]{:S(2)}, u32[]{:S(2)}) collective-permute-start(bf16[2,128,1152]{2,1,0:T(8,128)(2,1)S(1)} %get-tuple-element.58), channel_id=1, source_target_pairs={{0,24},{8,0},{16,8},{24,16},{1,25},{9,1},{17,9},{25,17},{2,26},{10... | collective-permute-start | bytes 1769480 | tf_op jit(solution)/shard_map/ppermute | solution.py:23
  46.2 9.7 %collective-permute-done.9.refs_2_ = bf16[2,144,1024]{2,1,0:T(8,128)(2,1)S(1)} collective-permute-done((bf16[2,144,1024]{2,1,0:T(8,128)(2,1)S(1)}, bf16[2,144,1024]{2,1,0:T(8,128)(2,1)S(1)}, u32[]{:S(2)}, u32[]{:S(2)}) %collective-permute-start.9) | collective-permute-done | bytes 589856 | tf_op jit(solution)/shard_map/ppermute | solution.py:23
  60.0 5.4 %shard_map.135 = (bf16[1,4,144,1024]{3,2,1,0:T(8,128)(2,1)S(1)}, bf16[1,4,144,1024]{3,2,1,0:T(8,128)(2,1)S(1)}) custom-call(s32[17]{0:T(128)S(1)} %stack.83.where_ref, bf16[1024,4608]{1,0:T(8,128)(2,1)} %left_ref.10, bf16[1024,1024]{1,0:T(8,128)(2,1)S(1)} %copy-done.1), custom_call_target="tpu_custom_call" | custom-call | flops 2415919104 | bytes 2359296 | tf_op jit(solution)/shard_map/pallas_call | solution.py:79
  67.0 2.6 %collective-permute-start.11 = (bf16[2,144,1024]{2,1,0:T(8,128)(2,1)S(1)}, bf16[2,144,1024]{2,1,0:T(8,128)(2,1)S(1)}, u32[]{:S(2)}, u32[]{:S(2)}) collective-permute-start(bf16[2,144,1024]{2,1,0:T(8,128)(2,1)S(1)} %get-tuple-element.66), channel_id=1, source_target_pairs={{0,96},{32,0},{64,32},{96,64},{1,97},{33,1},{65,33},{97,65},{2,98}... | collective-permute-start | bytes 1769480 | tf_op jit(solution)/shard_map/ppermute | solution.py:23
  69.9 6.1 %shard_map.139 = (bf16[1,4,128,1152]{3,2,1,0:T(8,128)(2,1)S(1)}, bf16[1,4,128,1152]{3,2,1,0:T(8,128)(2,1)S(1)}) custom-call(s32[17]{0:T(128)S(1)} %stack.83.where_ref, bf16[1024,4096]{1,0:T(8,128)(2,1)} %left_ref.11, bf16[1024,1152]{1,0:T(8,128)(2,1)S(1)} %copy-done), custom_call_target="tpu_custom_call" | custom-call | flops 2415919104 | bytes 2097152 | tf_op jit(solution)/shard_map/pallas_call | solution.py:79
  78.5 3.8 %collective-permute-done.11.refs_3_ = bf16[2,144,1024]{2,1,0:T(8,128)(2,1)S(1)} collective-permute-done((bf16[2,144,1024]{2,1,0:T(8,128)(2,1)S(1)}, bf16[2,144,1024]{2,1,0:T(8,128)(2,1)S(1)}, u32[]{:S(2)}, u32[]{:S(2)}) %collective-permute-start.11) | collective-permute-done | bytes 589856 | tf_op jit(solution)/shard_map/ppermute | solution.py:23
  82.2 1.6 collective-permute-start.19
  83.8 11.0 %collective-permute-done.8.refs_3_ = bf16[2,144,1024]{2,1,0:T(8,128)(2,1)S(1)} collective-permute-done((bf16[2,144,1024]{2,1,0:T(8,128)(2,1)S(1)}, bf16[2,144,1024]{2,1,0:T(8,128)(2,1)S(1)}, u32[]{:S(2)}, u32[]{:S(2)}) %collective-permute-start.8) | collective-permute-done | bytes 589856 | tf_op jit(solution)/shard_map/ppermute | solution.py:23
  94.9 1.8 %collective-permute-start.20 = (bf16[2,128,1152]{2,1,0:T(8,128)(2,1)S(1)}, bf16[2,128,1152]{2,1,0:T(8,128)(2,1)S(1)}, u32[]{:S(2)}, u32[]{:S(2)}) collective-permute-start(bf16[2,128,1152]{2,1,0:T(8,128)(2,1)S(1)} %get-tuple-element.76), channel_id=1, source_target_pairs={{0,24},{8,0},{16,8},{24,16},{1,25},{9,1},{17,9},{25,17},{2,26},{10... | collective-permute-start | bytes 1769480 | tf_op jit(solution)/shard_map/ppermute | solution.py:23
  96.7 1.7 collective-permute-start.17
  100.6 8.5 %collective-permute-done.20.refs_3_ = bf16[2,128,1152]{2,1,0:T(8,128)(2,1)S(1)} collective-permute-done((bf16[2,128,1152]{2,1,0:T(8,128)(2,1)S(1)}, bf16[2,128,1152]{2,1,0:T(8,128)(2,1)S(1)}, u32[]{:S(2)}, u32[]{:S(2)}) %collective-permute-start.20) | collective-permute-done | bytes 589856 | tf_op jit(solution)/shard_map/ppermute | solution.py:23
  112.3 9.5 %collective-permute-done.17.refs_3_ = bf16[2,128,1152]{2,1,0:T(8,128)(2,1)S(1)} collective-permute-done((bf16[2,128,1152]{2,1,0:T(8,128)(2,1)S(1)}, bf16[2,128,1152]{2,1,0:T(8,128)(2,1)S(1)}, u32[]{:S(2)}, u32[]{:S(2)}) %collective-permute-start.17) | collective-permute-done | bytes 589856 | tf_op jit(solution)/shard_map/ppermute | solution.py:23
  121.8 2.2 %collective-permute-start.21 = (bf16[1,128,1152]{2,1,0:T(8,128)(2,1)S(1)}, bf16[1,128,1152]{2,1,0:T(8,128)(2,1)S(1)}, u32[]{:S(2)}, u32[]{:S(2)}) collective-permute-start(bf16[1,128,1152]{2,1,0:T(8,128)(2,1)S(1)} %get-tuple-element.77), channel_id=1, source_target_pairs={{0,64},{32,96},{64,0},{96,32},{1,65},{33,97},{65,1},{97,33},{2,66}... | collective-permute-start | bytes 884744 | tf_op jit(solution)/shard_map/ppermute | solution.py:23
  124.0 1.8 %collective-permute-start.22 = (bf16[1,128,1152]{2,1,0:T(8,128)(2,1)S(1)}, bf16[1,128,1152]{2,1,0:T(8,128)(2,1)S(1)}, u32[]{:S(2)}, u32[]{:S(2)}) collective-permute-start(bf16[1,128,1152]{2,1,0:T(8,128)(2,1)S(1)} %get-tuple-element.78), channel_id=1, source_target_pairs={{0,32},{32,64},{64,96},{96,0},{1,33},{33,65},{65,97},{97,1},{2,34}... | collective-permute-start | bytes 884744 | tf_op jit(solution)/shard_map/ppermute | solution.py:23
  127.1 7.4 %collective-permute-done.14 = bf16[1,144,1024]{2,1,0:T(8,128)(2,1)S(1)} collective-permute-done((bf16[1,144,1024]{2,1,0:T(8,128)(2,1)S(1)}, bf16[1,144,1024]{2,1,0:T(8,128)(2,1)S(1)}, u32[]{:S(2)}, u32[]{:S(2)}) %collective-permute-start.14) | collective-permute-done | bytes 294944 | tf_op jit(solution)/shard_map/ppermute | solution.py:23
  135.2 2.8 %collective-permute-start.25 = (f32[272]{0:T(512)S(1)}, f32[272]{0:T(512)S(1)}, u32[]{:S(2)}, u32[]{:S(2)}) collective-permute-start(f32[272]{0:T(512)S(1)} %pad_maximum_fusion), channel_id=1, source_target_pairs={{0,2},{1,3},{2,0},{3,1},{4,6},{5,7},{6,4},{7,5},{8,10},{9,11},{10,... | collective-permute-start | bytes 3272 | tf_op jit(solution)/shard_map/ppermute | solution.py:23
  140.7 1.7 collective-permute-done.24
  143.8 2.7 %concatenate.7 = f32[2180]{0:T(1024)S(1)} concatenate(f32[1024]{0:T(1024)S(1)} %get-tuple-element.81, f32[1152]{0:T(1024)S(1)} %get-tuple-element.83, f32[1]{0:T(128)} %bitcast.29, f32[1]{0:T(128)} %bitcast.30, f32[1]{0:T(128)} %bitcast.31, f32[1]{0:T(128)} %bitcast.32), dimensions={0} | concatenate | bytes 17440 | tf_op jit(solution)/shard_map/concatenate | solution.py:261
  146.6 26.2 %all_to_all.5 = f32[32,1,2180]{2,1,0:T(1,128)S(1)} all-to-all(f32[32,1,2180]{2,1,0:T(1,128)S(1)} %broadcast_in_dim.2), channel_id=1, replica_groups=mesh['row_0'=4,'row_1'=4,'row_2'=2,'col'=4] {'row_0','row_1','row_2'}, dimensions={0} | all-to-all | bytes 558080 | tf_op jit(solution)/shard_map/all_to_all | solution.py:263
  (86 shorter events, 29.9 us)
Async XLA Ops:
  7.3 7.7 %collective-permute-start = (bf16[1,4,144,1024]{3,2,1,0:T(8,128)(2,1)S(1)}, bf16[1,4,144,1024]{3,2,1,0:T(8,128)(2,1)S(1)}, u32[]{:S(2)}, u32[]{:S(2)}) collective-permute-start(bf16[1,4,144,1024]{3,2,1,0:T(8,128)(2,1)S(1)} %get-tuple-element.44), channel_id=1, source_target_pairs={{0,4},{4,0},{1,5},{5,1},{2,6},{6,2},{3,7},{7,3},{8,12},{12,8},{9,1... | collective-permute-start | bytes 3538952 | tf_op jit(solution)/shard_map/ppermute | solution.py:23
  28.4 29.1 %collective-permute-start.2 = (bf16[2,4,144,1024]{3,2,1,0:T(8,128)(2,1)S(1)}, bf16[2,4,144,1024]{3,2,1,0:T(8,128)(2,1)S(1)}, u32[]{:S(2)}, u32[]{:S(2)}) collective-permute-start(bf16[2,4,144,1024]{3,2,1,0:T(8,128)(2,1)S(1)} %get-tuple-element.52), channel_id=1, source_target_pairs={{0,4},{4,0},{1,5},{5,1},{2,6},{6,2},{3,7},{7,3},{8,12},{12,8},{9,1... | collective-permute-start | bytes 7077896 | tf_op jit(solution)/shard_map/ppermute | solution.py:23
  39.2 20.2 %collective-permute-start.4 = (bf16[2,4,128,1152]{3,2,1,0:T(8,128)(2,1)S(1)}, bf16[2,4,128,1152]{3,2,1,0:T(8,128)(2,1)S(1)}, u32[]{:S(2)}, u32[]{:S(2)}) collective-permute-start(bf16[2,4,128,1152]{3,2,1,0:T(8,128)(2,1)S(1)} %get-tuple-element.57), channel_id=1, source_target_pairs={{0,4},{4,0},{1,5},{5,1},{2,6},{6,2},{3,7},{7,3},{8,12},{12,8},{9,1... | collective-permute-start | bytes 7077896 | tf_op jit(solution)/shard_map/ppermute | solution.py:23
  39.6 16.3 %collective-permute-start.9 = (bf16[2,144,1024]{2,1,0:T(8,128)(2,1)S(1)}, bf16[2,144,1024]{2,1,0:T(8,128)(2,1)S(1)}, u32[]{:S(2)}, u32[]{:S(2)}) collective-permute-start(bf16[2,144,1024]{2,1,0:T(8,128)(2,1)S(1)} %get-tuple-element.45), channel_id=1, source_target_pairs={{0,32},{32,64},{64,96},{96,0},{1,33},{33,65},{65,97},{97,1},{2,34}... | collective-permute-start | bytes 1769480 | tf_op jit(solution)/shard_map/ppermute | solution.py:23
  41.1 17.8 %collective-permute-start.3 = (bf16[2,144,1024]{2,1,0:T(8,128)(2,1)S(1)}, bf16[2,144,1024]{2,1,0:T(8,128)(2,1)S(1)}, u32[]{:S(2)}, u32[]{:S(2)}) collective-permute-start(bf16[2,144,1024]{2,1,0:T(8,128)(2,1)S(1)} %get-tuple-element.53), channel_id=1, source_target_pairs={{0,96},{32,0},{64,32},{96,64},{1,97},{33,1},{65,33},{97,65},{2,98}... | collective-permute-start | bytes 1769480 | tf_op jit(solution)/shard_map/ppermute | solution.py:23
  42.5 16.9 %collective-permute-start.5 = (bf16[2,128,1152]{2,1,0:T(8,128)(2,1)S(1)}, bf16[2,128,1152]{2,1,0:T(8,128)(2,1)S(1)}, u32[]{:S(2)}, u32[]{:S(2)}) collective-permute-start(bf16[2,128,1152]{2,1,0:T(8,128)(2,1)S(1)} %get-tuple-element.58), channel_id=1, source_target_pairs={{0,24},{8,0},{16,8},{24,16},{1,25},{9,1},{17,9},{25,17},{2,26},{10... | collective-permute-start | bytes 1769480 | tf_op jit(solution)/shard_map/ppermute | solution.py:23
  55.9 20.0 %collective-permute-start.18 = (bf16[2,128,1152]{2,1,0:T(8,128)(2,1)S(1)}, bf16[2,128,1152]{2,1,0:T(8,128)(2,1)S(1)}, u32[]{:S(2)}, u32[]{:S(2)}) collective-permute-start(bf16[2,128,1152]{2,1,0:T(8,128)(2,1)S(1)} %get-tuple-element.49), channel_id=1, source_target_pairs={{0,8},{8,16},{16,24},{24,0},{1,9},{9,17},{17,25},{25,1},{2,10},{10... | collective-permute-start | bytes 1769480 | tf_op jit(solution)/shard_map/ppermute | solution.py:23
  58.8 17.8 %collective-permute-start.10 = (bf16[2,144,1024]{2,1,0:T(8,128)(2,1)}, bf16[2,144,1024]{2,1,0:T(8,128)(2,1)S(1)}, u32[]{:S(2)}, u32[]{:S(2)}) collective-permute-start(bf16[2,144,1024]{2,1,0:T(8,128)(2,1)} %get-tuple-element.65), channel_id=1, source_target_pairs={{0,32},{32,64},{64,96},{96,0},{1,33},{33,65},{65,97},{97,1},{2,34}... | collective-permute-start | bytes 1769480 | tf_op jit(solution)/shard_map/ppermute | solution.py:23
  65.3 33.1 %collective-permute-start.6 = (bf16[1,4,144,1024]{3,2,1,0:T(8,128)(2,1)S(1)}, bf16[1,4,144,1024]{3,2,1,0:T(8,128)(2,1)S(1)}, u32[]{:S(2)}, u32[]{:S(2)}) collective-permute-start(bf16[1,4,144,1024]{3,2,1,0:T(8,128)(2,1)S(1)} %get-tuple-element.62), channel_id=1, source_target_pairs={{0,4},{4,0},{1,5},{5,1},{2,6},{6,2},{3,7},{7,3},{8,12},{12,8},{9,1... | collective-permute-start | bytes 3538952 | tf_op jit(solution)/shard_map/ppermute | solution.py:23
  67.0 15.2 %collective-permute-start.11 = (bf16[2,144,1024]{2,1,0:T(8,128)(2,1)S(1)}, bf16[2,144,1024]{2,1,0:T(8,128)(2,1)S(1)}, u32[]{:S(2)}, u32[]{:S(2)}) collective-permute-start(bf16[2,144,1024]{2,1,0:T(8,128)(2,1)S(1)} %get-tuple-element.66), channel_id=1, source_target_pairs={{0,96},{32,0},{64,32},{96,64},{1,97},{33,1},{65,33},{97,65},{2,98}... | collective-permute-start | bytes 1769480 | tf_op jit(solution)/shard_map/ppermute | solution.py:23
  69.6 25.2 %collective-permute-start.8 = (bf16[2,144,1024]{2,1,0:T(8,128)(2,1)S(1)}, bf16[2,144,1024]{2,1,0:T(8,128)(2,1)S(1)}, u32[]{:S(2)}, u32[]{:S(2)}) collective-permute-start(bf16[2,144,1024]{2,1,0:T(8,128)(2,1)S(1)} %get-tuple-element.63), channel_id=1, source_target_pairs={{0,96},{32,0},{64,32},{96,64},{1,97},{33,1},{65,33},{97,65},{2,98}... | collective-permute-start | bytes 1769480 | tf_op jit(solution)/shard_map/ppermute | solution.py:23
  76.0 34.5 %collective-permute-start.15 = (bf16[1,4,128,1152]{3,2,1,0:T(8,128)(2,1)S(1)}, bf16[1,4,128,1152]{3,2,1,0:T(8,128)(2,1)S(1)}, u32[]{:S(2)}, u32[]{:S(2)}) collective-permute-start(bf16[1,4,128,1152]{3,2,1,0:T(8,128)(2,1)S(1)} %get-tuple-element.72), channel_id=1, source_target_pairs={{0,4},{4,0},{1,5},{5,1},{2,6},{6,2},{3,7},{7,3},{8,12},{12,8},{9,1... | collective-permute-start | bytes 3538952 | tf_op jit(solution)/shard_map/ppermute | solution.py:23
  76.7 20.0 %collective-permute-start.7 = (bf16[2,144,1024]{2,1,0:T(8,128)(2,1)S(1)}, bf16[2,144,1024]{2,1,0:T(8,128)(2,1)S(1)}, u32[]{:S(2)}, u32[]{:S(2)}) collective-permute-start(bf16[2,144,1024]{2,1,0:T(8,128)(2,1)S(1)} %get-tuple-element.54), channel_id=1, source_target_pairs={{0,32},{32,64},{64,96},{96,0},{1,33},{33,65},{65,97},{97,1},{2,34}... | collective-permute-start | bytes 1769480 | tf_op jit(solution)/shard_map/ppermute | solution.py:23
  82.2 16.6 %collective-permute-start.19 = (bf16[2,128,1152]{2,1,0:T(8,128)(2,1)S(1)}, bf16[2,128,1152]{2,1,0:T(8,128)(2,1)S(1)}, u32[]{:S(2)}, u32[]{:S(2)}) collective-permute-start(bf16[2,128,1152]{2,1,0:T(8,128)(2,1)S(1)} %get-tuple-element.75), channel_id=1, source_target_pairs={{0,8},{8,16},{16,24},{24,0},{1,9},{9,17},{17,25},{25,1},{2,10},{10... | collective-permute-start | bytes 1769480 | tf_op jit(solution)/shard_map/ppermute | solution.py:23
  94.9 14.3 %collective-permute-start.20 = (bf16[2,128,1152]{2,1,0:T(8,128)(2,1)S(1)}, bf16[2,128,1152]{2,1,0:T(8,128)(2,1)S(1)}, u32[]{:S(2)}, u32[]{:S(2)}) collective-permute-start(bf16[2,128,1152]{2,1,0:T(8,128)(2,1)S(1)} %get-tuple-element.76), channel_id=1, source_target_pairs={{0,24},{8,0},{16,8},{24,16},{1,25},{9,1},{17,9},{25,17},{2,26},{10... | collective-permute-start | bytes 1769480 | tf_op jit(solution)/shard_map/ppermute | solution.py:23
  96.7 25.1 %collective-permute-start.17 = (bf16[2,128,1152]{2,1,0:T(8,128)(2,1)S(1)}, bf16[2,128,1152]{2,1,0:T(8,128)(2,1)S(1)}, u32[]{:S(2)}, u32[]{:S(2)}) collective-permute-start(bf16[2,128,1152]{2,1,0:T(8,128)(2,1)S(1)} %get-tuple-element.73), channel_id=1, source_target_pairs={{0,24},{8,0},{16,8},{24,16},{1,25},{9,1},{17,9},{25,17},{2,26},{10... | collective-permute-start | bytes 1769480 | tf_op jit(solution)/shard_map/ppermute | solution.py:23
  98.4 25.5 %collective-permute-start.16 = (bf16[2,128,1152]{2,1,0:T(8,128)(2,1)S(1)}, bf16[2,128,1152]{2,1,0:T(8,128)(2,1)S(1)}, u32[]{:S(2)}, u32[]{:S(2)}) collective-permute-start(bf16[2,128,1152]{2,1,0:T(8,128)(2,1)S(1)} %get-tuple-element.59), channel_id=1, source_target_pairs={{0,8},{8,16},{16,24},{24,0},{1,9},{9,17},{17,25},{25,1},{2,10},{10... | collective-permute-start | bytes 1769480 | tf_op jit(solution)/shard_map/ppermute | solution.py:23
  98.9 27.3 %collective-permute-start.12 = (bf16[1,144,1024]{2,1,0:T(8,128)(2,1)S(1)}, bf16[1,144,1024]{2,1,0:T(8,128)(2,1)S(1)}, u32[]{:S(2)}, u32[]{:S(2)}) collective-permute-start(bf16[1,144,1024]{2,1,0:T(8,128)(2,1)S(1)} %get-tuple-element.67), channel_id=1, source_target_pairs={{0,16},{8,24},{16,0},{24,8},{1,17},{9,25},{17,1},{25,9},{2,18},{10... | collective-permute-start | bytes 884744 | tf_op jit(solution)/shard_map/ppermute | solution.py:23
  109.1 18.0 %collective-permute-start.13 = (bf16[1,144,1024]{2,1,0:T(8,128)(2,1)S(1)}, bf16[1,144,1024]{2,1,0:T(8,128)(2,1)S(1)}, u32[]{:S(2)}, u32[]{:S(2)}) collective-permute-start(bf16[1,144,1024]{2,1,0:T(8,128)(2,1)S(1)} %get-tuple-element.68), channel_id=1, source_target_pairs={{0,8},{8,16},{16,24},{24,0},{1,9},{9,17},{17,25},{25,1},{2,10},{10... | collective-permute-start | bytes 884744 | tf_op jit(solution)/shard_map/ppermute | solution.py:23
  110.4 24.0 %collective-permute-start.14 = (bf16[1,144,1024]{2,1,0:T(8,128)(2,1)S(1)}, bf16[1,144,1024]{2,1,0:T(8,128)(2,1)S(1)}, u32[]{:S(2)}, u32[]{:S(2)}) collective-permute-start(bf16[1,144,1024]{2,1,0:T(8,128)(2,1)S(1)} %get-tuple-element.69), channel_id=1, source_target_pairs={{0,24},{8,0},{16,8},{24,16},{1,25},{9,1},{17,9},{25,17},{2,26},{10... | collective-permute-start | bytes 884744 | tf_op jit(solution)/shard_map/ppermute | solution.py:23
  121.8 13.0 %collective-permute-start.21 = (bf16[1,128,1152]{2,1,0:T(8,128)(2,1)S(1)}, bf16[1,128,1152]{2,1,0:T(8,128)(2,1)S(1)}, u32[]{:S(2)}, u32[]{:S(2)}) collective-permute-start(bf16[1,128,1152]{2,1,0:T(8,128)(2,1)S(1)} %get-tuple-element.77), channel_id=1, source_target_pairs={{0,64},{32,96},{64,0},{96,32},{1,65},{33,97},{65,1},{97,33},{2,66}... | collective-permute-start | bytes 884744 | tf_op jit(solution)/shard_map/ppermute | solution.py:23
  124.0 10.8 %collective-permute-start.22 = (bf16[1,128,1152]{2,1,0:T(8,128)(2,1)S(1)}, bf16[1,128,1152]{2,1,0:T(8,128)(2,1)S(1)}, u32[]{:S(2)}, u32[]{:S(2)}) collective-permute-start(bf16[1,128,1152]{2,1,0:T(8,128)(2,1)S(1)} %get-tuple-element.78), channel_id=1, source_target_pairs={{0,32},{32,64},{64,96},{96,0},{1,33},{33,65},{65,97},{97,1},{2,34}... | collective-permute-start | bytes 884744 | tf_op jit(solution)/shard_map/ppermute | solution.py:23
  126.2 8.6 %collective-permute-start.23 = (bf16[1,128,1152]{2,1,0:T(8,128)(2,1)S(1)}, bf16[1,128,1152]{2,1,0:T(8,128)(2,1)S(1)}, u32[]{:S(2)}, u32[]{:S(2)}) collective-permute-start(bf16[1,128,1152]{2,1,0:T(8,128)(2,1)S(1)} %get-tuple-element.79), channel_id=1, source_target_pairs={{0,96},{32,0},{64,32},{96,64},{1,97},{33,1},{65,33},{97,65},{2,98}... | collective-permute-start | bytes 884744 | tf_op jit(solution)/shard_map/ppermute | solution.py:23
  135.2 5.4 %collective-permute-start.25 = (f32[272]{0:T(512)S(1)}, f32[272]{0:T(512)S(1)}, u32[]{:S(2)}, u32[]{:S(2)}) collective-permute-start(f32[272]{0:T(512)S(1)} %pad_maximum_fusion), channel_id=1, source_target_pairs={{0,2},{1,3},{2,0},{3,1},{4,6},{5,7},{6,4},{7,5},{8,10},{9,11},{10,... | collective-permute-start | bytes 3272 | tf_op jit(solution)/shard_map/ppermute | solution.py:23
  (13 other events, 124.3 us)
